TPU v7x, 128 devices: a whole 4x4x4 slice. The times are simulated.
128 devices in a mesh: rep: 1, emb: 64 (over z, y, x), model: 2 (over core).
Axes of the slice: x: 4, y: 4, z: 4, core: 2. Of those that a mesh axis runs over, the one named last changes fastest.
Arguments:
- x: bfloat16 [128, 8192], P('rep')
- Wq: bfloat16 [8192, 8192], P('emb', 'model')
- Wk: bfloat16 [8192, 256], replicated
- Wv: bfloat16 [8192, 256], replicated
- Wo: bfloat16 [8192, 8192], P('model', 'emb')
- Kc: bfloat16 [128, 4096, 256], P('rep')
- Vc: bfloat16 [128, 4096, 256], P('rep')
- lengths: int32 [128], P('rep')
Outputs:
- output 1: bfloat16 [128, 8192], P('rep')
- output 2: bfloat16 [128, 256], P('rep')
- output 3: bfloat16 [128, 256], P('rep')
All inputs are finite; a program needn't handle non-finite values.
Results may differ from a plain program's by a relative error of at most 0.00955071.
Values are sent between devices in bfloat16 or wider.
A program may use at most 1.5 GiB of HBM per device.

v0:
```python
import jax
import jax.numpy as jnp
from jax import lax
from jax.sharding import PartitionSpec as P


def _attend(q, K, V, kn, vn, lens):
    dh = q.shape[-1]
    t = K.shape[1]
    scale = dh ** -0.5
    s = jnp.einsum('bhd,btd->bht', q, K, preferred_element_type=jnp.float32) * scale
    valid = jnp.arange(t)[None, :] < lens[:, None]
    s = jnp.where(valid[:, None, :], s, -jnp.inf)
    sn = jnp.einsum('bhd,bd->bh', q, kn, preferred_element_type=jnp.float32) * scale
    m = jnp.maximum(jnp.max(s, axis=-1), sn)
    p = jnp.exp(s - m[..., None])
    pn = jnp.exp(sn - m)
    l = jnp.sum(p, axis=-1) + pn
    acc = jnp.einsum('bht,btd->bhd', p.astype(jnp.bfloat16), V, preferred_element_type=jnp.float32)
    acc = acc + pn.astype(jnp.bfloat16).astype(jnp.float32)[..., None] * vn.astype(jnp.float32)[:, None, :]
    return (acc / l[..., None]).astype(jnp.bfloat16)


def solution(mesh):
    ne = mesh.shape['emb']
    nm = mesh.shape['model']

    def local(x, Wq, Wk, Wv, Wo, Kc, Vc, lengths):
        b, d = x.shape
        de = Wq.shape[0]
        dh = Wk.shape[1]
        hl = Wq.shape[1] // dh
        be = b // ne
        bl = be // nm
        i = lax.axis_index('emb')
        j = lax.axis_index('model')
        xi = lax.dynamic_slice_in_dim(x, i * de, de, axis=1)
        qp = jnp.dot(xi, Wq, preferred_element_type=jnp.float32)
        q = lax.psum_scatter(qp, 'emb', scatter_dimension=0, tiled=True)
        q = q.astype(jnp.bfloat16).reshape(be, hl, dh)
        q = lax.all_to_all(q, 'model', 0, 1, tiled=True)
        k_new = jnp.dot(x, Wk, preferred_element_type=jnp.float32).astype(jnp.bfloat16)
        v_new = jnp.dot(x, Wv, preferred_element_type=jnp.float32).astype(jnp.bfloat16)
        start = i * be + j * bl
        K = lax.dynamic_slice_in_dim(Kc, start, bl, 0)
        V = lax.dynamic_slice_in_dim(Vc, start, bl, 0)
        kn = lax.dynamic_slice_in_dim(k_new, start, bl, 0)
        vn = lax.dynamic_slice_in_dim(v_new, start, bl, 0)
        lens = lax.dynamic_slice_in_dim(lengths, start, bl, 0)
        o = _attend(q, K, V, kn, vn, lens)
        o = lax.all_to_all(o, 'model', 1, 0, tiled=True)
        o = lax.all_gather(o, 'emb', axis=0, tiled=True)
        yp = jnp.dot(o.reshape(b, hl * dh), Wo, preferred_element_type=jnp.float32).astype(jnp.bfloat16)
        ys = lax.psum(yp, 'model')
        yi = (xi.astype(jnp.float32) + ys.astype(jnp.float32)).astype(jnp.bfloat16)
        y = lax.all_gather(yi, 'emb', axis=1, tiled=True)
        return y, k_new, v_new

    in_specs = (P('rep', None), P('emb', 'model'), P(), P(), P('model', 'emb'),
                P('rep', None, None), P('rep', None, None), P('rep'))
    out_specs = (P('rep', None), P('rep', None), P('rep', None))
    return jax.shard_map(local, mesh=mesh, in_specs=in_specs, out_specs=out_specs, check_vma=False)
```

profile of v0, /device:TPU:1, one launch (start us, length us, event | category | flops | bytes accessed | tf_op | source)
XLA Modules:
  0.0 545.1 jit_solution(15648101633722676930)
XLA Ops:
  7.2 0.0 copy-start
  7.2 1.2 copy-done
  8.4 2.5 fusion.23
  10.9 318.8 %all-reduce.2 = bf16[128,4096]{1,0:T(8,128)(2,1)} all-reduce(f32[128,4096]{1,0:T(8,128)} %fusion.23), channel_id=2, replica_groups=mesh['rep'=1,'emb'=64,'model'=2] {'emb'}, use_global_device_ids=true, to_apply=%region_0.0.clone | all-reduce | flops 524288 | bytes 3145728
  329.7 0.6 dynamic-slice
  330.9 0.9 dynamic-slice_convert_fusion
  331.8 0.6 copy.18
  332.4 59.6 %all-to-all-start = ((bf16[2,16,256]{2,1,0:T(8,128)(2,1)}), bf16[2,16,256]{2,1,0:T(8,128)(2,1)S(1)}, u32[]{:S(2)}, u32[]{:S(2)}) async-start(bf16[2,16,256]{2,1,0:T(8,128)(2,1)} %bitcast.49), calls=%async_computation | async-start | bytes 32768 | tf_op jit(solution)/shard_map/all_to_all | solution.py:41
  392.0 0.6 dynamic_slice.19
  392.6 0.7 iota_compare_fusion
  393.3 0.0 copy-start.2
  393.3 3.1 convolution_convert_fusion.1
  396.3 0.4 copy-done.2
  396.7 0.8 convolution_convert_fusion
  397.5 2.4 fusion.32
  400.0 0.1 convert_convert_fusion
  400.1 0.3 fusion.19
  400.4 2.1 fusion.15
  402.5 0.5 broadcast.23
  403.1 0.7 reduce.4
  403.8 3.5 all_to_all.21
  407.3 0.6 copy.13
  407.9 0.0 all-gather.3.cloned.1.call-update
  407.9 0.0 all-gather.5.cloned.1.call-start
  408.0 56.6 %all-gather.3.cloned.1.call-done = bf16[128,16,256]{2,1,0:T(8,128)(2,1)} async-done(((bf16[2,16,256]{2,1,0:T(8,128)(2,1)}), bf16[128,16,256]{2,1,0:T(8,128)(2,1)}) %all-gather.3.cloned.1.call-update) | async-done | bytes 1048592 | tf_op jit(solution)/shard_map/all_gather | solution.py:52
  464.6 1.7 copy.15
  466.3 0.4 convolution_convert_fusion.2
  466.7 5.8 %psum.7 = bf16[128,128]{1,0:T(8,128)(2,1)S(1)} all-reduce(bf16[128,128]{1,0:T(8,128)(2,1)S(1)} %convolution_convert_fusion.2), channel_id=1, replica_groups=mesh['rep'=1,'emb'=64,'model'=2] {'model'}, use_global_device_ids=true, to_apply=%region_3.4 | all-reduce | flops 16384 | bytes 65536 | tf_op jit(solution)/shard_map/psum | solution.py:54
  472.6 0.6 add_convert_fusion
  473.2 0.0 all-gather.5.cloned.1.call-update
  473.2 62.0 %all-gather.5.cloned.1.call-done = bf16[128,8192]{1,0:T(8,128)(2,1)} async-done(((bf16[128,128]{1,0:T(8,128)(2,1)}), bf16[128,8192]{1,0:T(8,128)(2,1)}) %all-gather.5.cloned.1.call-update) | async-done | bytes 2097168 | tf_op jit(solution)/shard_map/all_gather | solution.py:56
  535.2 3.1 copy.23
  (19 shorter events, 0.1 us)
Async XLA Ops:
  7.2 1.2 copy-start
  10.9 318.8 %copy-start.7 = (u32[128]{0:T(128)S(1)}, u32[128]{0:T(128)}, u32[]{:S(2)}) copy-start(u32[128]{0:T(128)} %constant.25) | copy-start | bytes 1540
  10.9 381.1 %copy-start.6 = (s32[128]{0:T(128)S(1)}, s32[128]{0:T(128)}, u32[]{:S(2)}) copy-start(s32[128]{0:T(128)} %param.15) | copy-start | bytes 1540
  10.9 382.3 %copy-start.1 = (bf16[128,8192]{1,0:T(8,128)(2,1)S(1)}, bf16[128,8192]{1,0:T(8,128)(2,1)}, u32[]{:S(2)}) copy-start(bf16[128,8192]{1,0:T(8,128)(2,1)} %param.8) | copy-start | bytes 6291460
  332.4 65.1 %all-to-all-start = ((bf16[2,16,256]{2,1,0:T(8,128)(2,1)}), bf16[2,16,256]{2,1,0:T(8,128)(2,1)S(1)}, u32[]{:S(2)}, u32[]{:S(2)}) async-start(bf16[2,16,256]{2,1,0:T(8,128)(2,1)} %bitcast.49), calls=%async_computation | async-start | bytes 32768 | tf_op jit(solution)/shard_map/all_to_all | solution.py:41
  392.0 72.6 %all-gather.3.cloned.1.call-start = ((), (), s32[]{:S(2)}) async-start(), calls=%async_computation.2 | async-start | bytes 1064960 | tf_op jit(solution)/shard_map/all_gather | solution.py:52
  393.3 3.5 copy-start.2
  396.7 3.2 copy-start.4
  397.5 5.0 copy-start.5
  407.9 127.3 %all-gather.5.cloned.1.call-start = ((), (), s32[]{:S(2)}) async-start(), calls=%async_computation.3 | async-start | bytes 2129920 | tf_op jit(solution)/shard_map/all_gather | solution.py:56
  464.6 1.7 copy-start.3
Sparse Core Ops, SparseCore 0:
  408.0 56.4 all-gather.2
  473.4 61.8 all-gather.4
where the time goes:
time: 547 us; the launch traced here: 545 us
  blocking collectives  328 us (60%)
  waiting for transfers between devices  119 us (22%)
  starting transfers between devices  59.7 us (11%)
  between operations  14.8 us (3%)
  matrix products  11.4 us (2%)
  local copies, waits for them, and re-layouts  10.3 us (2%)
    unnamed x1, blocking collectives  319 us
    all_gather x1, waiting for transfers between devices, local(): y = lax.all_gather(yi, 'emb', axis=1, tiled=True)  62 us
    all_to_all x1, starting transfers between devices, local(): q = lax.all_to_all(q, 'model', 0, 1, tiled=True)  59.6 us
    all_gather x1, waiting for transfers between devices, local(): o = lax.all_gather(o, 'emb', axis=0, tiled=True)  56.6 us
  transfers between devices with their start and end apart: 3, of which 2 were waited for; matrix products, arithmetic and copies ran while one was open for 1% of the time, Pallas kernels for 0%

commit v1 on v0

v1 whole, which is shorter than its diff:
```python
import functools

import jax
import jax.numpy as jnp
from jax import lax
from jax.experimental import pallas as pl
from jax.experimental.pallas import tpu as pltpu
from jax.sharding import PartitionSpec as P

F32 = jnp.float32
BF16 = jnp.bfloat16
L = 128


def _kernel(side, nm, x_h, wq_h, wk_h, wv_h, wo_h, kc_h, vc_h, len_s,
            y_h, kn_o, vn_o,
            x_v, xi_v, wq_v, wkv_v, wo_v, k_v, v_v,
            qp, rq, kva, s_v, o_v, og, t_v, yp, yx, yb, y_v,
            sem_l, sem_out, s_q, r_q, s_o, r_o, s_e, r_e, s_y, r_y, s_f, r_f):
    ne = side ** 3
    n = ne * nm
    B, D = x_v.shape
    DE = xi_v.shape[1]
    CQ = wq_v.shape[1]
    NT = CQ // L
    DH = k_v.shape[1]
    HL = CQ // DH
    T = k_v.shape[0]
    DC = wo_v.shape[1]
    bh = B // nm
    scale = DH ** -0.5

    e = lax.axis_index('emb')
    m = lax.axis_index('model')
    z, y, x = e // (side * side), (e // side) % side, e % side
    me = e * nm + m

    def peer(d):
        dm = d % nm
        c = d // nm
        pz = (z + c // (side * side)) % side
        py = (y + (c // side) % side) % side
        px = (x + c % side) % side
        pe = (pz * side + py) * side + px
        return pe, (m + dm) % nm, dm

    bar = pltpu.get_barrier_semaphore()

    @pl.loop(1, n)
    def _(d):
        pe, pm, _dm = peer(d)
        pl.semaphore_signal(bar, inc=1, device_id={'emb': pe, 'model': pm})

    col = pl.multiple_of(e * DE, DE)
    loads = [
        pltpu.make_async_copy(x_h.at[:, pl.ds(col, DE)], xi_v, sem_l.at[0]),
        pltpu.make_async_copy(wq_h, wq_v, sem_l.at[1]),
        pltpu.make_async_copy(x_h, x_v, sem_l.at[2]),
        pltpu.make_async_copy(wk_h, wkv_v.at[0], sem_l.at[3]),
        pltpu.make_async_copy(wv_h, wkv_v.at[1], sem_l.at[4]),
        pltpu.make_async_copy(kc_h.at[me], k_v, sem_l.at[5]),
        pltpu.make_async_copy(vc_h.at[me], v_v, sem_l.at[6]),
        pltpu.make_async_copy(wo_h, wo_v, sem_l.at[7]),
    ]
    for c in loads:
        c.start()
    loads[0].wait()
    loads[1].wait()

    GN = 4
    for j0 in range(0, NT, GN):
        t = jnp.dot(xi_v[...], wq_v[:, j0 * L:(j0 + GN) * L], preferred_element_type=F32)
        for u in range(GN):
            j = j0 + u
            per = DH // L
            row = (j % per) * HL + j // per
            qp[pl.ds(row, B, stride=NT), :] = t[:, u * L:(u + 1) * L]

    pl.semaphore_wait(bar, n - 1)

    @pl.loop(1, n)
    def _(d):
        pe, pm, _dm = peer(d)
        b = pe * nm + pm
        pltpu.make_async_remote_copy(
            src_ref=qp.at[pl.ds(pl.multiple_of(b * NT, NT), NT)],
            dst_ref=rq.at[pl.ds(pl.multiple_of(d * NT, NT), NT)],
            send_sem=s_q, recv_sem=r_q,
            device_id={'emb': pe, 'model': pm},
        ).start()

    loads[2].wait()
    loads[3].wait()
    loads[4].wait()
    KB = min(1024, D)
    kva[...] = jnp.zeros_like(kva)

    @pl.loop(0, D // KB)
    def _(kk):
        o = pl.multiple_of(kk * KB, KB)
        xs = x_v[:, pl.ds(o, KB)]
        kva[0] += jnp.dot(xs, wkv_v[0, pl.ds(o, KB), :], preferred_element_type=F32)
        kva[1] += jnp.dot(xs, wkv_v[1, pl.ds(o, KB), :], preferred_element_type=F32)

    kn_o[...] = kva[0].astype(BF16)
    vn_o[...] = kva[1].astype(BF16)
    loads[5].wait()
    loads[6].wait()

    rest = rq.at[pl.ds(NT, (n - 1) * NT)]
    pltpu.make_async_copy(rest, rest, r_q).wait()

    own = qp[pl.ds(pl.multiple_of(me * NT, NT), NT), :]

    def add(c, acc):
        a0, a1 = acc
        base = pl.multiple_of(c * nm * NT, NT)
        return (a0 + rq[pl.ds(base, NT), :], a1 + rq[pl.ds(base + NT, NT), :])

    a0, a1 = lax.fori_loop(1, ne, add, (own, rq[pl.ds(NT, NT), :]))
    per = DH // L
    q = jnp.concatenate(
        [jnp.concatenate([a[u * HL:(u + 1) * HL] for u in range(per)], axis=1) for a in (a0, a1)],
        axis=0).astype(BF16)

    kn = kva[0, pl.ds(me, 1), :].astype(BF16).astype(F32)
    vn = kva[1, pl.ds(me, 1), :].astype(BF16).astype(F32)
    sn = jnp.sum(q.astype(F32) * kn, axis=1, keepdims=True) * scale
    ln = len_s[me]
    TB = min(1024, T)
    mx = sn
    for t0 in range(0, T, TB):
        s = lax.dot_general(q, k_v[t0:t0 + TB, :], (((1,), (1,)), ((), ())),
                            preferred_element_type=F32) * scale
        pos = lax.broadcasted_iota(jnp.int32, s.shape, 1) + t0
        s = jnp.where(pos < ln, s, -jnp.inf)
        s_v[:, t0:t0 + TB] = s
        mx = jnp.maximum(mx, jnp.max(s, axis=1, keepdims=True))
    pn = jnp.exp(sn - mx)
    l = pn
    acc = pn.astype(BF16).astype(F32) * vn
    for t0 in range(0, T, TB):
        p = jnp.exp(s_v[:, t0:t0 + TB] - mx)
        l = l + jnp.sum(p, axis=1, keepdims=True)
        acc = acc + jnp.dot(p.astype(BF16), v_v[t0:t0 + TB, :], preferred_element_type=F32)
    o_v[...] = (acc / l).astype(BF16).reshape(nm, HL, DH)

    @pl.loop(1, n)
    def _(d):
        pe, pm, dm = peer(d)
        pltpu.make_async_remote_copy(
            src_ref=o_v.at[dm], dst_ref=og.at[me], send_sem=s_o, recv_sem=r_o,
            device_id={'emb': pe, 'model': pm},
        ).start()

    og[me] = o_v[0]
    loads[7].wait()
    most = og.at[pl.ds(0, n - 1)]
    pltpu.make_async_copy(most, most, r_o).wait()

    @pl.loop(0, B)
    def _(b):
        v = og[b].astype(F32)
        r = pl.multiple_of(b * HL, HL)
        for u in range(per):
            t_v[u, pl.ds(r, HL), :] = v[:, u * L:(u + 1) * L]

    ya = jnp.zeros((B, DC), F32)
    for h in range(HL):
        lhs = jnp.concatenate(
            [t_v[u, pl.ds(h, B, stride=HL), :] for u in range(per)], axis=1).astype(BF16)
        ya = ya + jnp.dot(lhs, wo_v[h * DH:(h + 1) * DH, :], preferred_element_type=F32)
    yp[...] = ya

    om = (m + 1) % nm
    ex = pltpu.make_async_remote_copy(
        src_ref=yp.at[pl.ds(pl.multiple_of(om * bh, bh), bh)], dst_ref=yx, send_sem=s_e, recv_sem=r_e,
        device_id={'emb': e, 'model': om})
    ex.start()
    ex.wait_recv()
    rows = pl.ds(pl.multiple_of(m * bh, bh), bh)
    yb[...] = (xi_v[rows, :].astype(F32) + (yp[rows, :] + yx[...])).astype(BF16)

    ycol = pl.ds(pl.multiple_of(e * DC, DC), DC)

    @pl.loop(1, ne)
    def _(c):
        pe, pm, _dm = peer(c * nm)
        pltpu.make_async_remote_copy(
            src_ref=yb, dst_ref=y_v.at[rows, ycol], send_sem=s_y, recv_sem=r_y,
            device_id={'emb': pe, 'model': pm},
        ).start()

    y_v[rows, ycol] = yb[...]
    got = y_v.at[pl.ds(0, bh), pl.ds(0, (ne - 1) * DC)]
    pltpu.make_async_copy(got, got, r_y).wait()
    fw = pltpu.make_async_remote_copy(
        src_ref=y_v.at[rows], dst_ref=y_v.at[rows], send_sem=s_f, recv_sem=r_f,
        device_id={'emb': e, 'model': om})
    fw.start()
    out0 = pltpu.make_async_copy(y_v.at[rows], y_h.at[rows], sem_out.at[0])
    out0.start()
    fw.wait_recv()
    orow = pl.ds(pl.multiple_of(om * bh, bh), bh)
    out1 = pltpu.make_async_copy(y_v.at[orow], y_h.at[orow], sem_out.at[1])
    out1.start()
    ex.wait_send()
    fw.wait_send()
    pltpu.make_async_copy(rest, rest, s_q).wait()
    pltpu.make_async_copy(most, most, s_o).wait()
    pltpu.make_async_copy(got, got, s_y).wait()
    out0.wait()
    out1.wait()


def solution(mesh):
    ne = mesh.shape['emb']
    nm = mesh.shape['model']
    side = round(ne ** (1 / 3))

    def local(x, Wq, Wk, Wv, Wo, Kc, Vc, lengths):
        B, D = x.shape
        DE, CQ = Wq.shape
        DH = Wk.shape[1]
        T = Kc.shape[1]
        HL = CQ // DH
        NT = CQ // L
        DC = Wo.shape[1]
        n = ne * nm
        vm = pltpu.VMEM
        dma = pltpu.SemaphoreType.DMA
        any_ = pl.BlockSpec(memory_space=pl.ANY)
        return pl.pallas_call(
            functools.partial(_kernel, side, nm),
            out_shape=(jax.ShapeDtypeStruct((B, D), BF16),
                       jax.ShapeDtypeStruct((B, DH), BF16),
                       jax.ShapeDtypeStruct((B, DH), BF16)),
            in_specs=[any_] * 7 + [pl.BlockSpec(memory_space=pltpu.SMEM)],
            out_specs=(any_, pl.BlockSpec(memory_space=vm), pl.BlockSpec(memory_space=vm)),
            scratch_shapes=[
                vm((B, D), BF16), vm((B, DE), BF16), vm((DE, CQ), BF16), vm((2, D, DH), BF16),
                vm((CQ, DC), BF16), vm((T, DH), BF16), vm((T, DH), BF16),
                vm((B * NT, L), F32), vm((n * NT, L), F32), vm((2, B, DH), F32),
                vm((nm * HL, T), F32), vm((nm, HL, DH), BF16), vm((B, HL, DH), BF16),
                vm((DH // L, B * HL, L), F32), vm((B, DC), F32), vm((B // nm, DC), F32),
                vm((B // nm, DC), BF16), vm((B, D), BF16),
                dma((8,)), dma((2,)), dma, dma, dma, dma, dma, dma, dma, dma, dma, dma,
            ],
            compiler_params=pltpu.CompilerParams(
                collective_id=0, has_side_effects=True, vmem_limit_bytes=60 * 1024 * 1024),
            name='step',
        )(x, Wq, Wk, Wv, Wo, Kc, Vc, lengths)

    in_specs = (P('rep', None), P('emb', 'model'), P(), P(), P('model', 'emb'),
                P('rep', None, None), P('rep', None, None), P('rep'))
    out_specs = (P('rep', None), P('rep', None), P('rep', None))
    return jax.shard_map(local, mesh=mesh, in_specs=in_specs, out_specs=out_specs, check_vma=False)
```

time: 547 us -> 95.5 us (0.17)
  blocking collectives: 328 us -> 0 us
  waiting for transfers between devices: 119 us -> 0 us
  Pallas kernels: 0 us -> 90.3 us
  starting transfers between devices: 59.7 us -> 0 us
  between operations: 14.8 us -> 0.66 us
  matrix products: 11.4 us -> 0 us
  local copies, waits for them, and re-layouts: 10.3 us -> 4.4 us
    unnamed x1 -> x0, blocking collectives: 319 us -> none
    all_gather x2 -> x0, waiting for transfers between devices: 119 us -> none  [the longest x1 62 us: local(): y = lax.all_gather(yi, 'emb', axis=1, tiled=True)]
    pallas_call x0 -> x1, Pallas kernels: none -> 90.3 us  [local(): pl.pallas_call(functools.partial(_kernel, side, nm), out_shape=(jax.Shape...]
    all_to_all x1 -> x0, starting transfers between devices: 59.6 us -> none  [local(): q = lax.all_to_all(q, 'model', 0, 1, tiled=True)]
    dot_general x7 -> x0, matrix products: 11.4 us -> none  [the longest x1 3.05 us: local(): jnp.dot(x, Wk, preferred_element_type=jnp.float32).astype(jnp.bfloat16)]
    psum x1 -> x0, blocking collectives: 5.83 us -> none  [local(): ys = lax.psum(yp, 'model')]
  transfers between devices with their start and end apart: 3 -> 0, of which waited for: 2 -> 0; matrix products, arithmetic and copies ran while one was open for 1% -> 0% of each run, Pallas kernels for 0% -> 0%
where the time goes in v1:
time: 95.5 us; the launch traced here: 95.4 us
  Pallas kernels  90.3 us (95%)
  local copies, waits for them, and re-layouts  4.4 us (5%)
    pallas_call x1, Pallas kernels, local(): pl.pallas_call(functools.partial(_kernel, side, nm), out_shape=(jax.Shape...  90.3 us
    unnamed x7, local copies, waits for them, and re-layouts  4.4 us

profile of v1, /device:TPU:1, one launch (start us, length us, event | category | flops | bytes accessed | tf_op | source)
XLA Modules:
  0.0 95.4 jit_solution(9605939709678175482)
XLA Ops:
  0.6 90.3 %step.1 = (bf16[128,8192]{1,0:T(8,128)(2,1)}, bf16[128,256]{1,0:T(8,128)(2,1)}, bf16[128,256]{1,0:T(8,128)(2,1)}) custom-call(bf16[128,8192]{1,0:T(8,128)(2,1)} %x_h.1, bf16[128,4096]{1,0:T(8,128)(2,1)} %wq_h.1, bf16[8192,256]{1,0:T(8,128)(2,1)} %wk_h.1, bf16[8192,256]{1,0:T(8,128)(2,1)} %wv_h.1, bf16[4096,128]{1,0:T(8,128)(2,1)} %wo_h.1, ...), custom_call_target="tpu_custom_call" | custom-call | tf_op jit(solution)/shard_map/step/pallas_call | solution.py:233
  90.9 0.0 copy-start.1
  90.9 0.0 copy-start
  91.0 3.1 %copy.14 = bf16[128,8192]{1,0:T(8,128)(2,1)} copy(bf16[128,8192]{1,0:T(8,128)(2,1)} %get-tuple-element.6) | data formatting | bytes 4194304
  94.1 0.0 copy-done.1
  94.1 0.6 copy.15
  94.7 0.0 copy-done
  94.7 0.6 copy.16
Async XLA Ops:
  90.9 3.2 %copy-start.1 = (bf16[128,256]{1,0:T(8,128)(2,1)S(1)}, bf16[128,256]{1,0:T(8,128)(2,1)}, u32[]{:S(2)}) copy-start(bf16[128,256]{1,0:T(8,128)(2,1)} %get-tuple-element.7) | copy-start | bytes 196612
  90.9 3.8 %copy-start = (bf16[128,256]{1,0:T(8,128)(2,1)S(1)}, bf16[128,256]{1,0:T(8,128)(2,1)}, u32[]{:S(2)}) copy-start(bf16[128,256]{1,0:T(8,128)(2,1)} %get-tuple-element.8) | copy-start | bytes 196612

commit v2 on v0

v2 whole, which is shorter than its diff:
```python
import functools

import jax
import jax.numpy as jnp
from jax import lax
from jax.experimental import pallas as pl
from jax.experimental.pallas import tpu as pltpu
from jax.sharding import PartitionSpec as P

F32 = jnp.float32
BF16 = jnp.bfloat16
L = 128


def _kernel(side, nm, x_h, wq_h, wk_h, wv_h, wo_h, kc_h, vc_h, len_s,
            y_v, kn_o, vn_o,
            x_v, xl_v, wq_v, wx_v, wkv_v, wox_v, k_v, v_v,
            qp, rq, q_v, kva, s_v, of_v, os_v, og, t_v, yp, ys, ry, yb,
            sem_l, s_w, r_w, s_x, r_x, s_q, r_q, s_o, r_o, s_e, r_e, s_y, r_y, s_f, r_f):
    ne = side ** 3
    n = ne * nm
    B, D = x_v.shape
    DE = xl_v.shape[2]
    CQ = wq_v.shape[1]
    CB = CQ // side
    DH = k_v.shape[1]
    per = DH // L
    HB = CB // DH
    NB = CB // L
    RB = wox_v.shape[0]
    T = k_v.shape[0]
    DC = wo_h.shape[1]
    bh = B // nm
    scale = DH ** -0.5

    e = lax.axis_index('emb')
    m = lax.axis_index('model')
    z, y, x = e // (side * side), (e // side) % side, e % side
    me = e * nm + m

    def chip(cz, cy, cx):
        return (cz * side + cy) * side + cx

    xs = [(x + k) % side for k in range(side)]
    ms = [(m + k) % nm for k in range(nm)]
    zy = side * side

    def plane(t):
        pz = lax.rem(z + lax.div(t, side), side)
        return pz, (pz * side + lax.rem(y + lax.rem(t, side), side)) * side

    def everyone(send):
        def group(t, skip):
            pz, base = plane(t)
            for k in range(side):
                for dm in range(nm):
                    if not skip or k or dm:
                        send((t * side + k) * nm + dm, dm, pz, base + xs[k], ms[dm])

        @pl.loop(1, zy)
        def _(u):
            group(lax.rem(u * 5, zy), False)

        group(jnp.int32(0), True)

    def line(k):
        kx, ky = k * (1 - m), k * m
        pos = (x + kx) % side * (1 - m) + (y + ky) % side * m
        return chip(z, (y + ky) % side, (x + kx) % side), pos

    bar = pltpu.get_barrier_semaphore()

    everyone(lambda d, dm, pz, pe, pm: pl.semaphore_signal(
        bar, inc=1, device_id={'emb': pe, 'model': pm}))

    loads = [
        pltpu.make_async_copy(wq_h, wq_v, sem_l.at[0]),
        pltpu.make_async_copy(x_h, x_v, sem_l.at[1]),
        pltpu.make_async_copy(wk_h, wkv_v.at[0], sem_l.at[2]),
        pltpu.make_async_copy(wv_h, wkv_v.at[1], sem_l.at[3]),
        pltpu.make_async_copy(kc_h.at[me], k_v, sem_l.at[4]),
        pltpu.make_async_copy(vc_h.at[me], v_v, sem_l.at[5]),
        pltpu.make_async_copy(wo_h.at[pl.ds(pl.multiple_of(z * RB, RB), RB)], wox_v.at[:, pl.ds(0, DC)],
                              sem_l.at[6]),
    ]
    xl = []
    for k in range(side):
        src, _pos = line((side - k) % side)
        xl.append(pltpu.make_async_copy(
            x_h.at[:, pl.ds(pl.multiple_of(src * DE, DE), DE)], xl_v.at[k], sem_l.at[7 + k]))
    loads[0].start()
    for c in xl:
        c.start()
    for c in loads[1:]:
        c.start()
    loads[0].wait()

    pl.semaphore_wait(bar, n - 1)

    wsend = []
    for k in range(1, side):
        pe, pos = line(k)
        wsend.append(pltpu.make_async_remote_copy(
            src_ref=wq_v.at[:, pl.ds(pl.multiple_of(pos * CB, CB), CB)], dst_ref=wx_v.at[k],
            send_sem=s_w.at[k], recv_sem=r_w.at[k], device_id={'emb': pe, 'model': m}))
    for c in wsend:
        c.start()
    xsend = []
    for k in range(1, side):
        pz = (z + k) % side
        xsend.append(pltpu.make_async_remote_copy(
            src_ref=wo_h.at[pl.ds(pl.multiple_of(pz * RB, RB), RB)], dst_ref=wox_v.at[:, pl.ds(k * DC, DC)],
            send_sem=s_x.at[k], recv_sem=r_x.at[k], device_id={'emb': chip(pz, y, x), 'model': m}))
    for c in xsend:
        c.start()

    loads[1].wait()
    loads[2].wait()
    loads[3].wait()
    KB = min(1024, D)
    kva[...] = jnp.zeros_like(kva)

    @pl.loop(0, D // KB)
    def _(kk):
        o = pl.multiple_of(kk * KB, KB)
        xs = x_v[:, pl.ds(o, KB)]
        kva[0] += jnp.dot(xs, wkv_v[0, pl.ds(o, KB), :], preferred_element_type=F32)
        kva[1] += jnp.dot(xs, wkv_v[1, pl.ds(o, KB), :], preferred_element_type=F32)

    kn_o[...] = kva[0].astype(BF16)
    vn_o[...] = kva[1].astype(BF16)

    for c in xl:
        c.wait()
    _e, pos0 = line(0)
    for c in wsend:
        c.wait_recv()
    GN = min(4, NB)
    for j0 in range(0, NB, GN):
        t = jnp.dot(xl_v[0], wq_v[:, pl.ds(pl.multiple_of(pos0 * CB + j0 * L, L), GN * L)],
                    preferred_element_type=F32)
        for k in range(1, side):
            t = t + jnp.dot(xl_v[k], wx_v[k, :, j0 * L:(j0 + GN) * L], preferred_element_type=F32)
        for u in range(GN):
            j = j0 + u
            row = (j % per) * HB + j // per
            qp[pl.ds(row, B, stride=NB), :] = t[:, u * L:(u + 1) * L]

    def send_q(d, dm, pz, pe, pm):
        b = pe * nm + pm
        pltpu.make_async_remote_copy(
            src_ref=qp.at[pl.ds(pl.multiple_of(b * NB, NB), NB)],
            dst_ref=rq.at[pl.ds(pl.multiple_of(d * NB, NB), NB)],
            send_sem=s_q, recv_sem=r_q, device_id={'emb': pe, 'model': pm},
        ).start()

    everyone(send_q)

    rq[0:NB, :] = qp[pl.ds(pl.multiple_of(me * NB, NB), NB), :]
    loads[4].wait()
    loads[5].wait()
    rest = rq.at[pl.ds(NB, (n - 1) * NB)]
    pltpu.make_async_copy(rest, rest, r_q).wait()

    for s in range(nm):
        dm = (m + nm - s) % nm
        for j in range(side):
            acc = None
            for a in range(side):
                for b in range(side):
                    c = (a * side + b) * side + j if s == 0 else (a * side + j) * side + b
                    v = rq[pl.ds(pl.multiple_of((c * nm + dm) * NB, NB), NB), :]
                    acc = v if acc is None else acc + v
            r0 = (s * side + j) * HB
            for u in range(per):
                q_v[r0:r0 + HB, u * L:(u + 1) * L] = acc[u * HB:(u + 1) * HB]
    q = q_v[...].astype(BF16)

    kn = kva[0, pl.ds(me, 1), :].astype(BF16).astype(F32)
    vn = kva[1, pl.ds(me, 1), :].astype(BF16).astype(F32)
    sn = jnp.sum(q.astype(F32) * kn, axis=1, keepdims=True) * scale
    ln = len_s[me]
    TB = min(1024, T)
    mx = sn
    for t0 in range(0, T, TB):
        s = lax.dot_general(q, k_v[t0:t0 + TB, :], (((1,), (1,)), ((), ())),
                            preferred_element_type=F32) * scale
        tpos = lax.broadcasted_iota(jnp.int32, s.shape, 1) + t0
        s = jnp.where(tpos < ln, s, -jnp.inf)
        s_v[:, t0:t0 + TB] = s
        mx = jnp.maximum(mx, jnp.max(s, axis=1, keepdims=True))
    pn = jnp.exp(sn - mx)
    l = pn
    acc = pn.astype(BF16).astype(F32) * vn
    for t0 in range(0, T, TB):
        p = jnp.exp(s_v[:, t0:t0 + TB] - mx)
        l = l + jnp.sum(p, axis=1, keepdims=True)
        acc = acc + jnp.dot(p.astype(BF16), v_v[t0:t0 + TB, :], preferred_element_type=F32)
    o = acc / l
    for i in range(nm * side):
        for u in range(per):
            of_v[i * NB + u * HB:i * NB + (u + 1) * HB, :] = o[i * HB:(i + 1) * HB, u * L:(u + 1) * L]
    os_v[...] = of_v[...].reshape(nm * side, NB, L).astype(BF16)

    home = [x * (1 - pm) + y * pm + side for pm in ms]

    def send_o(d, dm, pz, pe, pm):
        pltpu.make_async_remote_copy(
            src_ref=os_v.at[pm * side + lax.rem(home[dm] - pz, side)], dst_ref=og.at[me],
            send_sem=s_o, recv_sem=r_o, device_id={'emb': pe, 'model': pm},
        ).start()

    everyone(send_o)
    og[me] = os_v[m * side + lax.rem(home[0] - z, side)]
    loads[6].wait()
    for c in xsend:
        c.wait_recv()
    most = og.at[pl.ds(0, n - 1)]
    pltpu.make_async_copy(most, most, r_o).wait()

    t_v[...] = og[...].astype(F32).reshape(B * NB, L)
    ya = None
    for h in range(HB):
        lhs = jnp.concatenate(
            [t_v[pl.ds(u * HB + h, B, stride=NB), :] for u in range(per)], axis=1).astype(BF16)
        t = jnp.dot(lhs, wox_v[h * DH:(h + 1) * DH, :], preferred_element_type=F32)
        ya = t if ya is None else ya + t
    yp[...] = ya[:, :DC]
    for k in range(side):
        ys[k] = ya[:, k * DC:(k + 1) * DC].astype(BF16)

    for k in range(side):
        for dm in range(nm):
            if k or dm:
                pe = chip((z + side - k) % side, y, x)
                pm = (m + dm) % nm
                pltpu.make_async_remote_copy(
                    src_ref=ys.at[k, pl.ds(pl.multiple_of(pm * bh, bh), bh)], dst_ref=ry.at[k * nm + dm],
                    send_sem=s_e, recv_sem=r_e, device_id={'emb': pe, 'model': pm}).start()
    parts = ry.at[pl.ds(1, side * nm - 1)]
    pltpu.make_async_copy(parts, parts, r_e).wait()
    rows = pl.ds(pl.multiple_of(m * bh, bh), bh)
    tot = yp[rows, :]
    for k in range(1, side * nm):
        tot = tot + ry[k].astype(F32)
    yb[...] = (xl_v[0, rows, :].astype(F32) + tot).astype(BF16)

    ycol = pl.ds(pl.multiple_of(e * DC, DC), DC)

    om = ms[1 % nm]
    hops = [side // 2] + [k for k in range(1, side) if k != side // 2] + [0]

    for dz in hops:
        def send_y(dy, _, dz=dz, skip=False):
            _pz, base = plane(dz * side + dy)
            for k in range(1 if skip else 0, side):
                pltpu.make_async_remote_copy(
                    src_ref=yb, dst_ref=y_v.at[rows, ycol], send_sem=s_y, recv_sem=r_y.at[dz],
                    device_id={'emb': base + xs[k], 'model': m},
                ).start()
            return 0

        lax.fori_loop(1 if dz == 0 else 0, side, send_y, 0)
        if dz == 0:
            send_y(jnp.int32(0), 0, skip=True)

    y_v[rows, ycol] = yb[...]
    fws = []
    for dz in hops:
        cnt = zy - (1 if dz == 0 else 0)
        got = y_v.at[pl.ds(0, bh), pl.ds(0, cnt * DC)]
        pltpu.make_async_copy(got, got, r_y.at[dz]).wait()
        cz = lax.rem(z + side - dz, side)
        span = y_v.at[rows, pl.ds(pl.multiple_of(cz * zy * DC, zy * DC), zy * DC)]
        fw = pltpu.make_async_remote_copy(
            src_ref=span, dst_ref=span, send_sem=s_f.at[dz], recv_sem=r_f.at[dz],
            device_id={'emb': e, 'model': om})
        fw.start()
        fws.append(fw)
    for c in wsend + xsend:
        c.wait_send()
    pltpu.make_async_copy(rest, rest, s_q).wait()
    pltpu.make_async_copy(most, most, s_o).wait()
    pltpu.make_async_copy(parts, parts, s_e).wait()
    allof = y_v.at[pl.ds(0, bh), pl.ds(0, (ne - 1) * DC)]
    pltpu.make_async_copy(allof, allof, s_y).wait()
    for fw in fws:
        fw.wait()


def _emit(*refs):
    k = (len(refs) - 1) // 2
    sem = refs[-1]
    cs = [pltpu.make_async_copy(refs[i], refs[k + i], sem.at[i]) for i in range(k)]
    for c in cs:
        c.start()
    for c in cs:
        c.wait()


def solution(mesh):
    ne = mesh.shape['emb']
    nm = mesh.shape['model']
    side = round(ne ** (1 / 3))

    def local(x, Wq, Wk, Wv, Wo, Kc, Vc, lengths):
        B, D = x.shape
        DE, CQ = Wq.shape
        DH = Wk.shape[1]
        T = Kc.shape[1]
        CB = CQ // side
        NB = CB // L
        HL = CQ // DH
        DC = Wo.shape[1]
        n = ne * nm
        bh = B // nm
        vm = pltpu.VMEM
        dma = pltpu.SemaphoreType.DMA
        any_ = pl.BlockSpec(memory_space=pltpu.HBM)
        vms = pl.BlockSpec(memory_space=vm)
        outs = ((B, D), (B, DH), (B, DH))
        res = pl.pallas_call(
            functools.partial(_kernel, side, nm),
            out_shape=tuple(vm(s, BF16) for s in outs),
            in_specs=[any_] * 7 + [pl.BlockSpec(memory_space=pltpu.SMEM)],
            out_specs=(vms, vms, vms),
            scratch_shapes=[
                vm((B, D), BF16), vm((side, B, DE), BF16), vm((DE, CQ), BF16), vm((side, DE, CB), BF16),
                vm((2, D, DH), BF16), vm((CB, side * DC), BF16), vm((T, DH), BF16), vm((T, DH), BF16),
                vm((B * NB, L), F32), vm((n * NB, L), F32), vm((nm * HL, DH), F32), vm((2, B, DH), F32),
                vm((nm * HL, T), F32), vm((nm * side * NB, L), F32), vm((nm * side, NB, L), BF16),
                vm((B, NB, L), BF16), vm((B * NB, L), F32), vm((B, DC), F32), vm((side, B, DC), BF16),
                vm((side * nm, bh, DC), BF16), vm((bh, DC), BF16),
                dma((7 + side,)), dma((side,)), dma((side,)), dma((side,)), dma((side,)),
                dma, dma, dma, dma, dma, dma, dma, dma((side,)), dma((side,)), dma((side,)),
            ],
            compiler_params=pltpu.CompilerParams(
                collective_id=0, has_side_effects=True, vmem_limit_bytes=61 * 1024 * 1024),
            name='step',
        )(x, Wq, Wk, Wv, Wo, Kc, Vc, lengths)
        return pl.pallas_call(
            _emit,
            out_shape=tuple(jax.ShapeDtypeStruct(s, BF16) for s in outs),
            in_specs=[vms] * 3,
            out_specs=(any_,) * 3,
            scratch_shapes=[dma((3,))],
            compiler_params=pltpu.CompilerParams(vmem_limit_bytes=1024 * 1024),
            name='emit',
        )(*[pltpu.with_memory_space_constraint(r, pltpu.VMEM) for r in res])

    in_specs = (P('rep', None), P('emb', 'model'), P(), P(), P('model', 'emb'),
                P('rep', None, None), P('rep', None, None), P('rep'))
    out_specs = (P('rep', None), P('rep', None), P('rep', None))
    return jax.shard_map(local, mesh=mesh, in_specs=in_specs, out_specs=out_specs, check_vma=False)
```

time: 547 us -> 63.4 us (0.12)
  blocking collectives: 328 us -> 0 us
  waiting for transfers between devices: 119 us -> 0 us
  Pallas kernels: 0 us -> 62.6 us
  starting transfers between devices: 59.7 us -> 0 us
  between operations: 14.8 us -> 0.64 us
  matrix products: 11.4 us -> 0 us
  local copies, waits for them, and re-layouts: 10.3 us -> 0 us
    unnamed x1 -> x0, blocking collectives: 319 us -> none
    all_gather x2 -> x0, waiting for transfers between devices: 119 us -> none  [the longest x1 62 us: local(): y = lax.all_gather(yi, 'emb', axis=1, tiled=True)]
    pallas_call x0 -> x2, Pallas kernels: none -> 62.6 us  [the longest x1 61.3 us: local(): pl.pallas_call(functools.partial(_kernel, side, nm), out_shape=tuple((vm(...]
    all_to_all x1 -> x0, starting transfers between devices: 59.6 us -> none  [local(): q = lax.all_to_all(q, 'model', 0, 1, tiled=True)]
    dot_general x7 -> x0, matrix products: 11.4 us -> none  [the longest x1 3.05 us: local(): jnp.dot(x, Wk, preferred_element_type=jnp.float32).astype(jnp.bfloat16)]
    unnamed x24 -> x0, local copies, waits for them, and re-layouts: 8.8 us -> none
    psum x1 -> x0, blocking collectives: 5.83 us -> none  [local(): ys = lax.psum(yp, 'model')]
  transfers between devices with their start and end apart: 3 -> 0, of which waited for: 2 -> 0; matrix products, arithmetic and copies ran while one was open for 1% -> 0% of each run, Pallas kernels for 0% -> 0%
where the time goes in v2:
time: 63.4 us; the launch traced here: 63.3 us
  Pallas kernels  62.6 us (99%)
  between operations  0.64 us (1%)
    pallas_call x1, Pallas kernels, local(): pl.pallas_call(functools.partial(_kernel, side, nm), out_shape=tuple((vm(...  61.3 us
    pallas_call x1, Pallas kernels, local(): pl.pallas_call(_emit, out_shape=tuple((jax.ShapeDtypeStruct(s, BF16) for...  1.37 us

profile of v2, /device:TPU:1, one launch (start us, length us, event | category | flops | bytes accessed | tf_op | source)
XLA Modules:
  0.0 63.3 jit_solution(7940146902330930533)
XLA Ops:
  0.6 61.3 %step.1 = (bf16[128,8192]{1,0:T(8,128)(2,1)S(1)}, bf16[128,256]{1,0:T(8,128)(2,1)S(1)}, bf16[128,256]{1,0:T(8,128)(2,1)S(1)}) custom-call(bf16[128,8192]{1,0:T(8,128)(2,1)} %x_h.1, bf16[128,4096]{1,0:T(8,128)(2,1)} %wq_h.1, bf16[8192,256]{1,0:T(8,128)(2,1)} %wk_h.1, bf16[8192,256]{1,0:T(8,128)(2,1)} %wv_h.1, bf16[4096,128]{1,0:T(8,128)(2,1)} %wo_h.1, ...), custom_call_target="tpu_custom_call" | custom-call | tf_op jit(solution)/shard_map/step/pallas_call | solution.py:322
  61.9 1.4 %emit.1 = (bf16[128,8192]{1,0:T(8,128)(2,1)}, bf16[128,256]{1,0:T(8,128)(2,1)}, bf16[128,256]{1,0:T(8,128)(2,1)}) custom-call(bf16[128,8192]{1,0:T(8,128)(2,1)S(1)} %get-tuple-element.6.refs_0_, bf16[128,256]{1,0:T(8,128)(2,1)S(1)} %get-tuple-element.7.refs_1_, bf16[128,256]{1,0:T(8,128)(2,1)S(1)} %get-tuple-element.8.refs_2_), custom_call_target="tpu_custom_call" | custom-call | tf_op jit(solution)/shard_map/emit/pallas_call | solution.py:341

commit v3 on v2

--- a/solution.py
+++ b/solution.py
@@ -16,7 +16,7 @@
             y_v, kn_o, vn_o,
             x_v, xl_v, wq_v, wx_v, wkv_v, wox_v, k_v, v_v,
             qp, rq, q_v, kva, s_v, of_v, os_v, og, t_v, yp, ys, ry, yb,
-            sem_l, s_w, r_w, s_x, r_x, s_q, r_q, s_o, r_o, s_e, r_e, s_y, r_y, s_f, r_f):
+            sem_l, s_w, r_w, s_x, r_x, s_q, r_q, s_o, r_o, s_e, r_e, s_y, r_y, r_z, s_f, r_f, s_b):
     ne = side ** 3
     n = ne * nm
     B, D = x_v.shape
@@ -70,8 +70,17 @@
 
     bar = pltpu.get_barrier_semaphore()
 
-    everyone(lambda d, dm, pz, pe, pm: pl.semaphore_signal(
-        bar, inc=1, device_id={'emb': pe, 'model': pm}))
+    def greet(sem, pe, pm):
+        pl.semaphore_signal(sem, inc=1, device_id={'emb': pe, 'model': pm})
+
+    ly = [chip(z, lax.rem(y + k, side), x) for k in range(1, side)]
+    lz = [chip(lax.rem(z + k, side), y, x) for k in range(1, side)]
+    for k in range(side):
+        for dm in range(nm):
+            if k or dm:
+                greet(bar, chip(z, y, xs[k]), ms[dm])
+    for pe in ly + lz:
+        greet(bar, pe, m)
 
     loads = [
         pltpu.make_async_copy(wq_h, wq_v, sem_l.at[0]),
@@ -95,7 +104,7 @@
         c.start()
     loads[0].wait()
 
-    pl.semaphore_wait(bar, n - 1)
+    pl.semaphore_wait(bar, side * nm - 1 + 2 * (side - 1))
 
     wsend = []
     for k in range(1, side):
@@ -113,6 +122,11 @@
             send_sem=s_x.at[k], recv_sem=r_x.at[k], device_id={'emb': chip(pz, y, x), 'model': m}))
     for c in xsend:
         c.start()
+    for pe in ly:
+        greet(s_b.at[0], pe, m)
+    pl.semaphore_wait(s_b.at[0], side - 1)
+    for pe in lz:
+        greet(s_b.at[1], pe, m)
 
     loads[1].wait()
     loads[2].wait()
@@ -130,6 +144,7 @@
     kn_o[...] = kva[0].astype(BF16)
     vn_o[...] = kva[1].astype(BF16)
 
+    pl.semaphore_wait(s_b.at[1], side - 1)
     for c in xl:
         c.wait()
     _e, pos0 = line(0)
@@ -248,32 +263,63 @@
     ycol = pl.ds(pl.multiple_of(e * DC, DC), DC)
 
     om = ms[1 % nm]
-    hops = [side // 2] + [k for k in range(1, side) if k != side // 2] + [0]
-
-    for dz in hops:
-        def send_y(dy, _, dz=dz, skip=False):
-            _pz, base = plane(dz * side + dy)
-            for k in range(1 if skip else 0, side):
-                pltpu.make_async_remote_copy(
-                    src_ref=yb, dst_ref=y_v.at[rows, ycol], send_sem=s_y, recv_sem=r_y.at[dz],
-                    device_id={'emb': base + xs[k], 'model': m},
-                ).start()
+    rb = min(8, bh // 8)
+    cuts = [0, (bh // rb + 2) // 3 * rb]
+    cuts += [min(bh, cuts[1] * 2), bh]
+    far = [side // 2] + [k for k in range(1, side) if k != side // 2]
+    here = (z, y, x)
+
+    def move(offs):
+        c = [h if o is None else lax.rem(h + side + o, side) for h, o in zip(here, offs)]
+        return chip(*c)
+
+    def offsets(axis, da, db, dl):
+        o = [da, db]
+        o.insert(axis, dl)
+        return o
+
+    def piece(c, src):
+        return y_v.at[pl.ds(pl.multiple_of(m * bh + cuts[c], rb), cuts[c + 1] - cuts[c]),
+                      pl.ds(pl.multiple_of(src * DC, DC), DC)]
+
+    def mine(c):
+        return yb.at[pl.ds(cuts[c], cuts[c + 1] - cuts[c])]
+
+    def push(src_ref, dst_ref, sem, pe):
+        pltpu.make_async_remote_copy(
+            src_ref=src_ref, dst_ref=dst_ref, send_sem=s_y, recv_sem=sem,
+            device_id={'emb': pe, 'model': m}).start()
+
+    for da in far + [0]:
+        def spread(db, _, da=da):
+            for c in range(3):
+                push(mine(c), piece(c, e), r_y.at[c, da], move(offsets(c, da, db, None)))
             return 0
-
-        lax.fori_loop(1 if dz == 0 else 0, side, send_y, 0)
-        if dz == 0:
-            send_y(jnp.int32(0), 0, skip=True)
-
+        lax.fori_loop(1 if da == 0 else 0, side, spread, 0)
+    for c in range(3):
+        for dl in far:
+            push(mine(c), piece(c, e), r_z.at[c], move(offsets(c, None, None, dl)))
     y_v[rows, ycol] = yb[...]
+
+    for da in [0] + far[::-1]:
+        for c in range(3):
+            got = y_v.at[pl.ds(0, cuts[c + 1] - cuts[c]), pl.ds(0, (side - (da == 0)) * DC)]
+            pltpu.make_async_copy(got, got, r_y.at[c, da]).wait()
+
+            def relay(db, _, da=da, c=c):
+                ref = piece(c, move(offsets(c, -da, -db, None)))
+                for dl in far:
+                    push(ref, ref, r_z.at[c], move(offsets(c, None, None, dl)))
+                return 0
+            lax.fori_loop(1 if da == 0 else 0, side, relay, 0)
+
     fws = []
-    for dz in hops:
-        cnt = zy - (1 if dz == 0 else 0)
-        got = y_v.at[pl.ds(0, bh), pl.ds(0, cnt * DC)]
-        pltpu.make_async_copy(got, got, r_y.at[dz]).wait()
-        cz = lax.rem(z + side - dz, side)
-        span = y_v.at[rows, pl.ds(pl.multiple_of(cz * zy * DC, zy * DC), zy * DC)]
+    for c in range(3):
+        got = y_v.at[pl.ds(0, cuts[c + 1] - cuts[c]), pl.ds(0, (side - 1) * zy * DC)]
+        pltpu.make_async_copy(got, got, r_z.at[c]).wait()
+        span = y_v.at[pl.ds(pl.multiple_of(m * bh + cuts[c], rb), cuts[c + 1] - cuts[c])]
         fw = pltpu.make_async_remote_copy(
-            src_ref=span, dst_ref=span, send_sem=s_f.at[dz], recv_sem=r_f.at[dz],
+            src_ref=span, dst_ref=span, send_sem=s_f.at[c], recv_sem=r_f.at[c],
             device_id={'emb': e, 'model': om})
         fw.start()
         fws.append(fw)
@@ -332,7 +378,8 @@
                 vm((B, NB, L), BF16), vm((B * NB, L), F32), vm((B, DC), F32), vm((side, B, DC), BF16),
                 vm((side * nm, bh, DC), BF16), vm((bh, DC), BF16),
                 dma((7 + side,)), dma((side,)), dma((side,)), dma((side,)), dma((side,)),
-                dma, dma, dma, dma, dma, dma, dma, dma((side,)), dma((side,)), dma((side,)),
+                dma, dma, dma, dma, dma, dma, dma, dma((3, side)), dma((3,)), dma((3,)), dma((3,)),
+                pltpu.SemaphoreType.REGULAR((2,)),
             ],
             compiler_params=pltpu.CompilerParams(
                 collective_id=0, has_side_effects=True, vmem_limit_bytes=61 * 1024 * 1024),

time: 63.4 us -> 57.8 us (0.912)
  Pallas kernels: 62.6 us -> 57.1 us
    pallas_call x1, Pallas kernels: 61.3 us -> 55.7 us  [local(): pl.pallas_call(functools.partial(_kernel, side, nm), out_shape=tuple((vm(...]
where the time goes in v3:
time: 57.8 us; the launch traced here: 57.7 us
  Pallas kernels  57.1 us (99%)
  between operations  0.64 us (1%)
    pallas_call x1, Pallas kernels, local(): pl.pallas_call(functools.partial(_kernel, side, nm), out_shape=tuple((vm(...  55.7 us
    pallas_call x1, Pallas kernels, local(): pl.pallas_call(_emit, out_shape=tuple((jax.ShapeDtypeStruct(s, BF16) for...  1.37 us

profile of v3, /device:TPU:1, one launch (start us, length us, event | category | flops | bytes accessed | tf_op | source)
XLA Modules:
  0.0 57.7 jit_solution(14331561260345869340)
XLA Ops:
  0.6 55.7 %step.1 = (bf16[128,8192]{1,0:T(8,128)(2,1)S(1)}, bf16[128,256]{1,0:T(8,128)(2,1)S(1)}, bf16[128,256]{1,0:T(8,128)(2,1)S(1)}) custom-call(bf16[128,8192]{1,0:T(8,128)(2,1)} %x_h.1, bf16[128,4096]{1,0:T(8,128)(2,1)} %wq_h.1, bf16[8192,256]{1,0:T(8,128)(2,1)} %wk_h.1, bf16[8192,256]{1,0:T(8,128)(2,1)} %wv_h.1, bf16[4096,128]{1,0:T(8,128)(2,1)} %wo_h.1, ...), custom_call_target="tpu_custom_call" | custom-call | tf_op jit(solution)/shard_map/step/pallas_call | solution.py:368
  56.3 1.4 %emit.1 = (bf16[128,8192]{1,0:T(8,128)(2,1)}, bf16[128,256]{1,0:T(8,128)(2,1)}, bf16[128,256]{1,0:T(8,128)(2,1)}) custom-call(bf16[128,8192]{1,0:T(8,128)(2,1)S(1)} %get-tuple-element.6.refs_0_, bf16[128,256]{1,0:T(8,128)(2,1)S(1)} %get-tuple-element.7.refs_1_, bf16[128,256]{1,0:T(8,128)(2,1)S(1)} %get-tuple-element.8.refs_2_), custom_call_target="tpu_custom_call" | custom-call | tf_op jit(solution)/shard_map/emit/pallas_call | solution.py:388

commit v4 on v3

--- a/solution.py
+++ b/solution.py
@@ -27,6 +27,10 @@
     per = DH // L
     HB = CB // DH
     NB = CB // L
+    NC = qp.shape[0]
+    CC = CB // NC
+    HC = HB // NC
+    RC = NB // NC
     RB = wox_v.shape[0]
     T = k_v.shape[0]
     DC = wo_h.shape[1]
@@ -44,6 +48,7 @@
     xs = [(x + k) % side for k in range(side)]
     ms = [(m + k) % nm for k in range(nm)]
     zy = side * side
+    far = [side // 2] + [k for k in range(1, side) if k != side // 2]
 
     def plane(t):
         pz = lax.rem(z + lax.div(t, side), side)
@@ -107,11 +112,13 @@
     pl.semaphore_wait(bar, side * nm - 1 + 2 * (side - 1))
 
     wsend = []
-    for k in range(1, side):
-        pe, pos = line(k)
-        wsend.append(pltpu.make_async_remote_copy(
-            src_ref=wq_v.at[:, pl.ds(pl.multiple_of(pos * CB, CB), CB)], dst_ref=wx_v.at[k],
-            send_sem=s_w.at[k], recv_sem=r_w.at[k], device_id={'emb': pe, 'model': m}))
+    for h in range(NC):
+        for k in far:
+            pe, pos = line(k)
+            wsend.append(pltpu.make_async_remote_copy(
+                src_ref=wq_v.at[:, pl.ds(pl.multiple_of(pos * CB + h * CC, CC), CC)],
+                dst_ref=wx_v.at[k, :, pl.ds(h * CC, CC)],
+                send_sem=s_w.at[h, k], recv_sem=r_w.at[h, k], device_id={'emb': pe, 'model': m}))
     for c in wsend:
         c.start()
     xsend = []
@@ -148,47 +155,44 @@
     for c in xl:
         c.wait()
     _e, pos0 = line(0)
-    for c in wsend:
-        c.wait_recv()
-    GN = min(4, NB)
-    for j0 in range(0, NB, GN):
-        t = jnp.dot(xl_v[0], wq_v[:, pl.ds(pl.multiple_of(pos0 * CB + j0 * L, L), GN * L)],
+    for h in range(NC):
+        for c in wsend[h * (side - 1):(h + 1) * (side - 1)]:
+            c.wait_recv()
+        t = jnp.dot(xl_v[0], wq_v[:, pl.ds(pl.multiple_of(pos0 * CB + h * CC, CC), CC)],
                     preferred_element_type=F32)
         for k in range(1, side):
-            t = t + jnp.dot(xl_v[k], wx_v[k, :, j0 * L:(j0 + GN) * L], preferred_element_type=F32)
-        for u in range(GN):
-            j = j0 + u
-            row = (j % per) * HB + j // per
-            qp[pl.ds(row, B, stride=NB), :] = t[:, u * L:(u + 1) * L]
-
-    def send_q(d, dm, pz, pe, pm):
-        b = pe * nm + pm
-        pltpu.make_async_remote_copy(
-            src_ref=qp.at[pl.ds(pl.multiple_of(b * NB, NB), NB)],
-            dst_ref=rq.at[pl.ds(pl.multiple_of(d * NB, NB), NB)],
-            send_sem=s_q, recv_sem=r_q, device_id={'emb': pe, 'model': pm},
-        ).start()
-
-    everyone(send_q)
-
-    rq[0:NB, :] = qp[pl.ds(pl.multiple_of(me * NB, NB), NB), :]
+            t = t + jnp.dot(xl_v[k], wx_v[k, :, h * CC:(h + 1) * CC], preferred_element_type=F32)
+        for j in range(RC):
+            qp[h, :, (j % per) * HC + j // per, :] = t[:, j * L:(j + 1) * L]
+
+        def send_q(d, dm, pz, pe, pm, h=h):
+            pltpu.make_async_remote_copy(
+                src_ref=qp.at[h, pe * nm + pm], dst_ref=rq.at[h, d],
+                send_sem=s_q, recv_sem=r_q.at[h], device_id={'emb': pe, 'model': pm},
+            ).start()
+
+        everyone(send_q)
+        rq[h, 0] = qp[h, me]
+
     loads[4].wait()
     loads[5].wait()
-    rest = rq.at[pl.ds(NB, (n - 1) * NB)]
-    pltpu.make_async_copy(rest, rest, r_q).wait()
+    for h in range(NC):
+        rest = rq.at[h, pl.ds(1, n - 1)]
+        pltpu.make_async_copy(rest, rest, r_q.at[h]).wait()
 
     for s in range(nm):
         dm = (m + nm - s) % nm
         for j in range(side):
-            acc = None
-            for a in range(side):
-                for b in range(side):
-                    c = (a * side + b) * side + j if s == 0 else (a * side + j) * side + b
-                    v = rq[pl.ds(pl.multiple_of((c * nm + dm) * NB, NB), NB), :]
-                    acc = v if acc is None else acc + v
-            r0 = (s * side + j) * HB
-            for u in range(per):
-                q_v[r0:r0 + HB, u * L:(u + 1) * L] = acc[u * HB:(u + 1) * HB]
+            for h in range(NC):
+                acc = None
+                for a in range(side):
+                    for b in range(side):
+                        c = (a * side + b) * side + j if s == 0 else (a * side + j) * side + b
+                        v = rq[h, c * nm + dm]
+                        acc = v if acc is None else acc + v
+                r0 = (s * side + j) * HB + h * HC
+                for u in range(per):
+                    q_v[r0:r0 + HC, u * L:(u + 1) * L] = acc[u * HC:(u + 1) * HC]
     q = q_v[...].astype(BF16)
 
     kn = kva[0, pl.ds(me, 1), :].astype(BF16).astype(F32)
@@ -244,7 +248,7 @@
     for k in range(side):
         ys[k] = ya[:, k * DC:(k + 1) * DC].astype(BF16)
 
-    for k in range(side):
+    for k in far + [0]:
         for dm in range(nm):
             if k or dm:
                 pe = chip((z + side - k) % side, y, x)
@@ -266,7 +270,6 @@
     rb = min(8, bh // 8)
     cuts = [0, (bh // rb + 2) // 3 * rb]
     cuts += [min(bh, cuts[1] * 2), bh]
-    far = [side // 2] + [k for k in range(1, side) if k != side // 2]
     here = (z, y, x)
 
     def move(offs):
@@ -298,7 +301,7 @@
         lax.fori_loop(1 if da == 0 else 0, side, spread, 0)
     for c in range(3):
         for dl in far:
-            push(mine(c), piece(c, e), r_z.at[c], move(offsets(c, None, None, dl)))
+            push(mine(c), piece(c, e), r_z.at[c, dl], move(offsets(c, None, None, dl)))
     y_v[rows, ycol] = yb[...]
 
     for da in [0] + far[::-1]:
@@ -309,35 +312,54 @@
             def relay(db, _, da=da, c=c):
                 ref = piece(c, move(offsets(c, -da, -db, None)))
                 for dl in far:
-                    push(ref, ref, r_z.at[c], move(offsets(c, None, None, dl)))
+                    push(ref, ref, r_z.at[c, dl], move(offsets(c, None, None, dl)))
                 return 0
             lax.fori_loop(1 if da == 0 else 0, side, relay, 0)
 
-    fws = []
+    def cross(c, dl):
+        at = lax.rem(here[c] + side - dl, side)
+        width = side ** (2 - c) * DC
+
+        def one(g, _):
+            ref = y_v.at[pl.ds(pl.multiple_of(m * bh + cuts[c], rb), cuts[c + 1] - cuts[c]),
+                         pl.ds(pl.multiple_of((g * side + at) * width, width), width)]
+            pltpu.make_async_remote_copy(
+                src_ref=ref, dst_ref=ref, send_sem=s_f, recv_sem=r_f,
+                device_id={'emb': e, 'model': om}).start()
+            return 0
+
+        lax.fori_loop(0, side ** c, one, 0)
+
     for c in range(3):
-        got = y_v.at[pl.ds(0, cuts[c + 1] - cuts[c]), pl.ds(0, (side - 1) * zy * DC)]
-        pltpu.make_async_copy(got, got, r_z.at[c]).wait()
-        span = y_v.at[pl.ds(pl.multiple_of(m * bh + cuts[c], rb), cuts[c + 1] - cuts[c])]
-        fw = pltpu.make_async_remote_copy(
-            src_ref=span, dst_ref=span, send_sem=s_f.at[c], recv_sem=r_f.at[c],
-            device_id={'emb': e, 'model': om})
-        fw.start()
-        fws.append(fw)
+        cross(c, 0)
+    for dl in far[::-1]:
+        for c in range(3):
+            got = y_v.at[pl.ds(0, cuts[c + 1] - cuts[c]), pl.ds(0, zy * DC)]
+            pltpu.make_async_copy(got, got, r_z.at[c, dl]).wait()
+            cross(c, dl)
     for c in wsend + xsend:
         c.wait_send()
-    pltpu.make_async_copy(rest, rest, s_q).wait()
+    allq = rq.at[:, pl.ds(1, n - 1)]
+    pltpu.make_async_copy(allq, allq, s_q).wait()
     pltpu.make_async_copy(most, most, s_o).wait()
     pltpu.make_async_copy(parts, parts, s_e).wait()
     allof = y_v.at[pl.ds(0, bh), pl.ds(0, (ne - 1) * DC)]
     pltpu.make_async_copy(allof, allof, s_y).wait()
-    for fw in fws:
-        fw.wait()
+    half = y_v.at[pl.ds(0, bh)]
+    pltpu.make_async_copy(half, half, s_f).wait()
+    pltpu.make_async_copy(half, half, r_f).wait()
 
 
 def _emit(*refs):
     k = (len(refs) - 1) // 2
     sem = refs[-1]
-    cs = [pltpu.make_async_copy(refs[i], refs[k + i], sem.at[i]) for i in range(k)]
+    cs = []
+    for i in range(k):
+        r = refs[i].shape[0]
+        q = r // 8 if i == 0 else r
+        for p in range(r // q):
+            rows = pl.ds(p * q, q)
+            cs.append(pltpu.make_async_copy(refs[i].at[rows], refs[k + i].at[rows], sem.at[len(cs)]))
     for c in cs:
         c.start()
     for c in cs:
@@ -356,6 +378,7 @@
         T = Kc.shape[1]
         CB = CQ // side
         NB = CB // L
+        NC = 1
         HL = CQ // DH
         DC = Wo.shape[1]
         n = ne * nm
@@ -373,12 +396,12 @@
             scratch_shapes=[
                 vm((B, D), BF16), vm((side, B, DE), BF16), vm((DE, CQ), BF16), vm((side, DE, CB), BF16),
                 vm((2, D, DH), BF16), vm((CB, side * DC), BF16), vm((T, DH), BF16), vm((T, DH), BF16),
-                vm((B * NB, L), F32), vm((n * NB, L), F32), vm((nm * HL, DH), F32), vm((2, B, DH), F32),
+                vm((NC, B, NB // NC, L), F32), vm((NC, n, NB // NC, L), F32), vm((nm * HL, DH), F32), vm((2, B, DH), F32),
                 vm((nm * HL, T), F32), vm((nm * side * NB, L), F32), vm((nm * side, NB, L), BF16),
                 vm((B, NB, L), BF16), vm((B * NB, L), F32), vm((B, DC), F32), vm((side, B, DC), BF16),
                 vm((side * nm, bh, DC), BF16), vm((bh, DC), BF16),
-                dma((7 + side,)), dma((side,)), dma((side,)), dma((side,)), dma((side,)),
-                dma, dma, dma, dma, dma, dma, dma, dma((3, side)), dma((3,)), dma((3,)), dma((3,)),
+                dma((7 + side,)), dma((NC, side)), dma((NC, side)), dma((side,)), dma((side,)),
+                dma, dma((NC,)), dma, dma, dma, dma, dma, dma((3, side)), dma((3, side)), dma, dma,
                 pltpu.SemaphoreType.REGULAR((2,)),
             ],
             compiler_params=pltpu.CompilerParams(
@@ -390,7 +413,7 @@
             out_shape=tuple(jax.ShapeDtypeStruct(s, BF16) for s in outs),
             in_specs=[vms] * 3,
             out_specs=(any_,) * 3,
-            scratch_shapes=[dma((3,))],
+            scratch_shapes=[dma((10,))],
             compiler_params=pltpu.CompilerParams(vmem_limit_bytes=1024 * 1024),
             name='emit',
         )(*[pltpu.with_memory_space_constraint(r, pltpu.VMEM) for r in res])

time: 57.8 us -> 56.8 us (0.983)
  Pallas kernels: 57.1 us -> 56.1 us
    pallas_call x1, Pallas kernels: 55.7 us -> 54.6 us  [local(): pl.pallas_call(functools.partial(_kernel, side, nm), out_shape=tuple((vm(...]
where the time goes in v4:
time: 56.8 us; the launch traced here: 56.7 us
  Pallas kernels  56.1 us (99%)
  between operations  0.64 us (1%)
    pallas_call x1, Pallas kernels, local(): pl.pallas_call(functools.partial(_kernel, side, nm), out_shape=tuple((vm(...  54.6 us
    pallas_call x1, Pallas kernels, local(): pl.pallas_call(_emit, out_shape=tuple((jax.ShapeDtypeStruct(s, BF16) for...  1.43 us

profile of v4, /device:TPU:1, one launch (start us, length us, event | category | flops | bytes accessed | tf_op | source)
XLA Modules:
  0.0 56.7 jit_solution(4754970296761685334)
XLA Ops:
  0.6 54.6 %step.1 = (bf16[128,8192]{1,0:T(8,128)(2,1)S(1)}, bf16[128,256]{1,0:T(8,128)(2,1)S(1)}, bf16[128,256]{1,0:T(8,128)(2,1)S(1)}) custom-call(bf16[128,8192]{1,0:T(8,128)(2,1)} %x_h.1, bf16[128,4096]{1,0:T(8,128)(2,1)} %wq_h.1, bf16[8192,256]{1,0:T(8,128)(2,1)} %wk_h.1, bf16[8192,256]{1,0:T(8,128)(2,1)} %wv_h.1, bf16[4096,128]{1,0:T(8,128)(2,1)} %wo_h.1, ...), custom_call_target="tpu_custom_call" | custom-call | tf_op jit(solution)/shard_map/step/pallas_call | solution.py:391
  55.3 1.4 %emit.1 = (bf16[128,8192]{1,0:T(8,128)(2,1)}, bf16[128,256]{1,0:T(8,128)(2,1)}, bf16[128,256]{1,0:T(8,128)(2,1)}) custom-call(bf16[128,8192]{1,0:T(8,128)(2,1)S(1)} %get-tuple-element.6.refs_0_, bf16[128,256]{1,0:T(8,128)(2,1)S(1)} %get-tuple-element.7.refs_1_, bf16[128,256]{1,0:T(8,128)(2,1)S(1)} %get-tuple-element.8.refs_2_), custom_call_target="tpu_custom_call" | custom-call | tf_op jit(solution)/shard_map/emit/pallas_call | solution.py:411
